TPU v7x, 64 devices: a 2x2x8 block of a 4x4x8 slice. The times are simulated.
64 devices in a mesh: dp: 4 (over x, y), ep: 16 (over z, core).
Axes of the slice: x: 2, y: 2, z: 8, core: 2. Of those that a mesh axis runs over, the one named last changes fastest.
The devices are a block of a 4x4x8 slice.
Arguments:
- tokens: bfloat16 [64, 1024, 768], P(('dp', 'ep')), parts along dimension 0
- w_gate: bfloat16 [768, 16], replicated
- expert_ids: int32 [64, 1024, 2], P(('dp', 'ep')), parts along dimension 0
- keep_second: int32 [64, 1024], P(('dp', 'ep')), parts along dimension 0
- w_in: bfloat16 [16, 768, 3072], P('ep')
- w_out: bfloat16 [16, 3072, 768], P('ep')
Outputs:
- output: bfloat16 [64, 1024, 768], P(('dp', 'ep')), parts along dimension 0
There are 4 independent parts. A program takes and returns all parts, laid end to end along the dimension named above; an argument that names none is the same for every part.
All inputs are finite; a program needn't handle non-finite values.
Results may differ from a plain program's by a relative error of at most 0.001.
Values are sent between devices in bfloat16 or wider.
A program may use at most 768 MiB of HBM per device.

v0:
```python
import jax
import jax.numpy as jnp
from jax import lax
from jax.sharding import PartitionSpec as P


def build_routing(tokens, w_gate, expert_ids, keep_second, capacity):
    expert_count = w_gate.shape[1]
    logits = jnp.einsum("gsm,me->gse", tokens, w_gate, preferred_element_type=jnp.float32)
    gate_probs = jax.nn.softmax(logits, axis=-1)
    first_hot = jax.nn.one_hot(expert_ids[:, :, 0], expert_count, dtype=jnp.int32)
    second_hot = jax.nn.one_hot(expert_ids[:, :, 1], expert_count, dtype=jnp.int32) * keep_second[:, :, None]
    gate_first = jnp.sum(gate_probs * first_hot, axis=-1)
    gate_second = jnp.sum(gate_probs * second_hot, axis=-1)
    gate_total = gate_first + gate_second
    pos_first = jnp.sum((jnp.cumsum(first_hot, axis=1) - first_hot) * first_hot, axis=-1)
    second_base = jnp.cumsum(second_hot, axis=1) - second_hot + jnp.sum(first_hot, axis=1, keepdims=True)
    pos_second = jnp.sum(second_base * second_hot, axis=-1)
    slot_first = first_hot.astype(jnp.bfloat16)[:, :, :, None] * jax.nn.one_hot(pos_first, capacity, dtype=jnp.bfloat16)[:, :, None, :]
    slot_second = second_hot.astype(jnp.bfloat16)[:, :, :, None] * jax.nn.one_hot(pos_second, capacity, dtype=jnp.bfloat16)[:, :, None, :]
    dispatch = slot_first + slot_second
    weight_first = (gate_first / gate_total).astype(jnp.bfloat16)[:, :, None, None]
    weight_second = (gate_second / gate_total).astype(jnp.bfloat16)[:, :, None, None]
    combine = weight_first * slot_first + weight_second * slot_second
    return dispatch, combine


def solution(mesh):
    group_count = mesh.shape["ep"]

    def local_layer(tokens, w_gate, expert_ids, keep_second, w_in, w_out):
        token_count = tokens.shape[1]
        model_dim = tokens.shape[2]
        expert_count = w_gate.shape[1]
        local_experts = w_in.shape[0]
        capacity = 2 * token_count // expert_count
        dispatch, combine = build_routing(tokens, w_gate, expert_ids, keep_second, capacity)
        send_rows = jnp.einsum("gsec,gsm->ecm", dispatch, tokens, preferred_element_type=jnp.float32).astype(jnp.bfloat16)
        send_rows = send_rows.reshape(group_count, local_experts, capacity, model_dim)
        recv_rows = lax.all_to_all(send_rows, "ep", 0, 0, tiled=True)
        hidden = jax.nn.relu(jnp.einsum("gecm,emh->egch", recv_rows, w_in, preferred_element_type=jnp.float32)).astype(jnp.bfloat16)
        back_rows = jnp.einsum("egch,ehm->gecm", hidden, w_out, preferred_element_type=jnp.float32).astype(jnp.bfloat16)
        back_rows = lax.all_to_all(back_rows, "ep", 0, 0, tiled=True)
        back_rows = back_rows.reshape(expert_count, capacity, model_dim)
        mixed_rows = jnp.einsum("gsec,ecm->gsm", combine, back_rows, preferred_element_type=jnp.float32)
        return mixed_rows.astype(jnp.bfloat16)

    group_spec = P(("dp", "ep"))
    return jax.shard_map(local_layer, mesh=mesh, in_specs=(group_spec, P(), group_spec, group_spec, P("ep"), P("ep")), out_specs=group_spec, check_vma=False)
```

profile of v0, /device:TPU:28, one launch (start us, length us, event | category | flops | bytes accessed | tf_op | source)
XLA Modules:
  0.0 215.4 jit_solution(10719600937206492360)
XLA Ops:
  0.0 0.0 copy-start
  0.0 0.8 fusion.57
  0.8 0.7 select_convert_fusion
  1.6 0.7 select_bitcast_fusion
  2.3 4.5 %reduce-window.16 = s32[1,16,8,128]{3,2,1,0:T(8,128)S(1)} reduce-window(s32[1,16,8,128]{3,2,1,0:T(8,128)S(1)} %bitcast.82, s32[]{:T(128)} %constant.14.clone.1), window={size=1x1x1x128 pad=0_0x0_0x0_0x127_0}, to_apply=%region_7.8 | reduce-window | flops 2080768 | bytes 131076 | tf_op jit(solution)/shard_map/reduce-window.2
  6.8 0.1 slice.26
  7.0 4.5 %reduce-window.14 = s32[1,16,8,128]{3,2,1,0:T(8,128)S(1)} reduce-window(s32[1,16,8,128]{3,2,1,0:T(8,128)S(1)} %bitcast.83, s32[]{:T(128)} %constant.14.clone.1), window={size=1x1x1x128 pad=0_0x0_0x0_0x127_0}, to_apply=%region_4.5 | reduce-window | flops 2080768 | bytes 131076 | tf_op jit(solution)/shard_map/reduce-window
  11.5 0.1 slice.24
  11.6 0.1 copy.14
  11.7 0.1 copy.15
  11.8 0.1 broadcast.222
  11.9 0.1 copy.12
  12.1 0.1 copy.13
  12.2 0.1 broadcast.220
  12.3 0.1 fusion.45
  12.4 0.8 fusion.51
  13.2 0.3 fusion.42
  13.5 0.0 copy-done
  13.5 8.6 %convert_bitcast_fusion.1 = bf16[16,1,128,768]{3,2,1,0:T(8,128)(2,1)S(1)} fusion(bf16[1024,128]{1,0:T(8,128)(2,1)S(1)} %get-tuple-element.16, bf16[1024,16]{0,1:T(8,128)(2,1)S(1)} %select_convert_fusion, bf16[1024,128]{1,0:T(8,128)(2,1)S(1)} %get-tuple-element.15, bf16[1024,16]{0,1:T(8,128)(2,1)S(1)} %convert_convert_fusion, ...), kind=kOutput, calls=%fused_computation.16 | convolution fusion | flops 3229089792 | bytes 5308416 | tf_op jit(solution)/shard_map/gsec,gsm->ecm/dot_general | solution.py:38
  22.2 82.0 %all_to_all.10 = bf16[16,1,128,768]{3,2,1,0:T(8,128)(2,1)} all-to-all(bf16[16,1,128,768]{3,2,1,0:T(8,128)(2,1)S(1)} %convert_bitcast_fusion.1), channel_id=1, replica_groups=mesh['dp'=4,'ep'=16] {'ep'}, dimensions={0} | all-to-all | bytes 6291456 | tf_op jit(solution)/shard_map/all_to_all | solution.py:40
  104.2 25.4 %convert_bitcast_fusion = bf16[16,1,128,768]{3,2,1,0:T(8,128)(2,1)} fusion(bf16[1,3072,768]{2,1,0:T(8,128)(2,1)} %param.11, bf16[1,768,3072]{2,1,0:T(8,128)(2,1)} %param.10, bf16[16,1,128,768]{3,2,1,0:T(8,128)(2,1)} %all_to_all.10), kind=kOutput, calls=%fused_computation.15 | convolution fusion | flops 19341508608 | bytes 15728640 | tf_op jit(solution)/shard_map/egch,ehm->gecm/dot_general | solution.py:42
  129.6 0.0 copy-start.2
  129.6 0.0 copy-start.1
  129.6 5.2 %all-to-all-start.1 = ((bf16[16,1,128,768]{3,2,1,0:T(8,128)(2,1)}), bf16[16,1,128,768]{3,2,1,0:T(8,128)(2,1)}, u32[]{:S(2)}, u32[]{:S(2)}) async-start(bf16[16,1,128,768]{3,2,1,0:T(8,128)(2,1)} %convert_bitcast_fusion), calls=%async_computation.1 | async-start | bytes 6291456 | tf_op jit(solution)/shard_map/all_to_all | solution.py:43
  134.8 0.0 copy-done.2
  134.8 0.5 fusion.58
  135.4 0.0 copy-done.1
  135.4 0.1 fusion.49
  135.5 69.9 %all-to-all-done.1 = bf16[16,1,128,768]{3,2,1,0:T(8,128)(2,1)} async-done(((bf16[16,1,128,768]{3,2,1,0:T(8,128)(2,1)}), bf16[16,1,128,768]{3,2,1,0:T(8,128)(2,1)}, u32[]{:S(2)}, u32[]{:S(2)}) %all-to-all-start.1) | async-done | bytes 3145760 | tf_op jit(solution)/shard_map/all_to_all | solution.py:43
  205.4 10.0 %fusion.37 = bf16[1,1024,768]{2,1,0:T(8,128)(2,1)} fusion(bf16[16,1,128,768]{3,2,1,0:T(8,128)(2,1)} %all-to-all-done.1, bf16[1024,128]{1,0:T(8,128)(2,1)S(1)} %get-tuple-element.16, bf16[1024,16]{0,1:T(8,128)(2,1)S(1)} %select_convert_fusion, bf16[1024]{0:T(1024)(128)(2,1)S(1)} %get-tuple-element.10, bf16[1024,128]{1,0:T(8,128)(2,1)S(1)} %get-tuple-element.15, ...), kind=kOutput, calls=%fused_computation.30 | convolution fusion | flops 3232497664 | bytes 5312512 | tf_op jit(solution)/shard_map/gsec,ecm->gsm/dot_general | solution.py:45
  (14 shorter events, 0.3 us)
Async XLA Ops:
  0.0 13.5 %copy-start = (bf16[1,1024,768]{2,1,0:T(8,128)(2,1)S(1)}, bf16[1,1024,768]{2,1,0:T(8,128)(2,1)}, u32[]{:S(2)}) copy-start(bf16[1,1024,768]{2,1,0:T(8,128)(2,1)} %param.6) | copy-start | bytes 4718596
  129.6 5.2 %copy-start.2 = (bf16[768,16]{0,1:T(8,128)(2,1)S(1)}, bf16[768,16]{0,1:T(8,128)(2,1)}, u32[]{:S(2)}) copy-start(bf16[768,16]{0,1:T(8,128)(2,1)} %param.7) | copy-start | bytes 73732
  129.6 5.8 %copy-start.1 = (s32[1,1024]{1,0:T(1,128)S(1)}, s32[1,1024]{1,0:T(1,128)}, u32[]{:S(2)}) copy-start(s32[1,1024]{1,0:T(1,128)} %param.9) | copy-start | bytes 12292
  129.6 75.8 %all-to-all-start.1 = ((bf16[16,1,128,768]{3,2,1,0:T(8,128)(2,1)}), bf16[16,1,128,768]{3,2,1,0:T(8,128)(2,1)}, u32[]{:S(2)}, u32[]{:S(2)}) async-start(bf16[16,1,128,768]{3,2,1,0:T(8,128)(2,1)} %convert_bitcast_fusion), calls=%async_computation.1 | async-start | bytes 6291456 | tf_op jit(solution)/shard_map/all_to_all | solution.py:43
where the time goes:
time: 216 us; the launch traced here: 215 us
  blocking collectives  82 us (38%)
  waiting for transfers between devices  69.9 us (32%)
  matrix products  44.6 us (21%)
  other arithmetic  11.8 us (5%)
  starting transfers between devices  5.2 us (2%)
    all_to_all x1, blocking collectives, local_layer(): recv_rows = lax.all_to_all(send_rows, 'ep', 0, 0, tiled=True)  82 us
    all_to_all x1, waiting for transfers between devices, local_layer(): back_rows = lax.all_to_all(back_rows, 'ep', 0, 0, tiled=True)  69.9 us
    dot_general x1, matrix products, local_layer(): jnp.einsum('egch,ehm->gecm', hidden, w_out, preferred_element_type=jnp.fl...  25.4 us
    dot_general x1, matrix products, local_layer(): jnp.einsum('gsec,ecm->gsm', combine, back_rows, preferred_element_type=jn...  10 us
    another operation x4, other arithmetic  9.09 us
    dot_general x1, matrix products, local_layer(): jnp.einsum('gsec,gsm->ecm', dispatch, tokens, preferred_element_type=jnp....  8.63 us
    all_to_all x1, starting transfers between devices, local_layer(): back_rows = lax.all_to_all(back_rows, 'ep', 0, 0, tiled=True)  5.2 us
  transfers between devices with their start and end apart: 1, of which 1 were waited for; matrix products, arithmetic and copies ran while one was open for 0% of the time, Pallas kernels for 0%

commit v1 on v0

v1 whole, which is shorter than its diff:
```python
import functools

import jax
import jax.numpy as jnp
from jax import lax
from jax.experimental import pallas as pl
from jax.experimental.pallas import tpu as pltpu
from jax.sharding import PartitionSpec as P

MESH = pl.DeviceIdType.MESH
CORES = 2
LANES = 128


def route_slots(ids_ref, keep_ref, experts, capacity):
    tokens = ids_ref.shape[1]
    first = ids_ref[0:1, :]
    second = ids_ref[1:2, :]
    keep = keep_ref[0:1, :]
    expert_row = lax.broadcasted_iota(jnp.int32, (experts, tokens), 0)
    first_hot = jnp.where(expert_row == first, 1.0, 0.0)
    second_hot = jnp.where((expert_row == second) & (keep == 1), 1.0, 0.0)
    hot = jnp.concatenate([first_hot, second_hot], axis=0)
    blocks = tokens // LANES
    stacked = jnp.concatenate([hot[:, b * LANES:(b + 1) * LANES] for b in range(blocks)], axis=0).astype(jnp.bfloat16)
    row = lax.broadcasted_iota(jnp.int32, (LANES, 2 * LANES), 0)
    col = lax.broadcasted_iota(jnp.int32, (LANES, 2 * LANES), 1)
    before = jnp.where((row < col) | (col >= LANES), 1.0, 0.0).astype(jnp.bfloat16)
    counts = jnp.dot(stacked, before, preferred_element_type=jnp.float32)
    rows = 2 * experts
    offset = jnp.zeros((rows, LANES), jnp.float32)
    prefix = []
    for b in range(blocks):
        part = counts[b * rows:(b + 1) * rows]
        prefix.append(part[:, :LANES] + offset)
        offset = offset + part[:, LANES:]
    first_total = offset[:experts]
    slot_first, slot_second = [], []
    for b in range(blocks):
        lanes = slice(b * LANES, (b + 1) * LANES)
        pos_first = jnp.sum(prefix[b][:experts] * first_hot[:, lanes], axis=0, keepdims=True)
        pos_second = jnp.sum((prefix[b][experts:] + first_total) * second_hot[:, lanes], axis=0, keepdims=True)
        slot_first.append(pos_first)
        slot_second.append(pos_second)
    pos_first = jnp.concatenate(slot_first, axis=1).astype(jnp.int32)
    pos_second = jnp.concatenate(slot_second, axis=1).astype(jnp.int32)
    slot_first = jnp.where(pos_first < capacity, first * capacity + pos_first, -1)
    slot_second = jnp.where((keep == 1) & (pos_second < capacity), second * capacity + pos_second, -1)
    return slot_first, slot_second, first_hot, second_hot


def layer_kernel(n, tokens_hbm, gate_ref, ids_ref, keep_ref, w_in_hbm, w_out_hbm, out_ref,
                 tokens_ref, w_in, w_out, send, recv, back, ret, hidden, combine, total, slots,
                 load_sem, send_sem, recv_sem, back_sem, ret_sem):
    me = lax.axis_index("ep")
    part = lax.axis_index("dp")
    chips = n // CORES
    chip = me // CORES
    core = lax.rem(me, CORES)
    experts = gate_ref.shape[0]
    tokens, model = tokens_ref.shape
    hid = w_in.shape[1]
    capacity = 2 * tokens // experts
    pair = CORES * capacity
    local = chips - 1

    load_tokens = pltpu.make_async_copy(tokens_hbm, tokens_ref, load_sem.at[0])
    load_in = pltpu.make_async_copy(w_in_hbm, w_in, load_sem.at[1])
    load_out = pltpu.make_async_copy(w_out_hbm, w_out, load_sem.at[2])
    load_tokens.start()
    load_in.start()
    load_out.start()

    barrier = pltpu.get_barrier_semaphore()
    for k in range(1, n):
        pl.semaphore_signal(barrier, inc=1, device_id=(part, lax.rem(me + k, n)), device_id_type=MESH)

    slot_first, slot_second, first_hot, second_hot = route_slots(ids_ref, keep_ref, experts, capacity)
    slots[0:1, :] = slot_first
    slots[1:2, :] = slot_second

    def offset_of(step):
        size = (chips - step) // 2
        return jnp.where(lax.rem(step, 2) == 1, size, chips - size)

    def target_chip(step):
        return lax.rem(chip + offset_of(step), chips)

    def source_chip(step):
        return lax.rem(chip + chips - offset_of(step), chips)

    def forward(step, c):
        return pltpu.make_async_remote_copy(
            src_ref=send.at[step, c], dst_ref=recv.at[step, core],
            send_sem=send_sem.at[step, c], recv_sem=recv_sem.at[step, core],
            device_id=(part, target_chip(step) * CORES + c), device_id_type=MESH)

    def arrived(step, c):
        return pltpu.make_async_remote_copy(
            src_ref=send.at[step, c], dst_ref=recv.at[step, c],
            send_sem=send_sem.at[step, c], recv_sem=recv_sem.at[step, c],
            device_id=(part, target_chip(step) * CORES + c), device_id_type=MESH)

    def reply(step, c):
        return pltpu.make_async_remote_copy(
            src_ref=back.at[step, c], dst_ref=ret.at[step, core],
            send_sem=back_sem.at[step, c], recv_sem=ret_sem.at[step, core],
            device_id=(part, source_chip(step) * CORES + c), device_id_type=MESH)

    def returned(step, c):
        return pltpu.make_async_remote_copy(
            src_ref=back.at[step, c], dst_ref=ret.at[step, c],
            send_sem=back_sem.at[step, c], recv_sem=ret_sem.at[step, c],
            device_id=(part, source_chip(step) * CORES + c), device_id_type=MESH)

    slot_row = lax.broadcasted_iota(jnp.int32, (pair, tokens), 0)

    def dispatch(step):
        base = target_chip(step) * pair
        hit = (slot_row == slots[0:1, :] - base) | (slot_row == slots[1:2, :] - base)
        pick = jnp.where(hit, 1.0, 0.0).astype(jnp.bfloat16)
        for c in range(CORES):
            rows = jnp.dot(pick[c * capacity:(c + 1) * capacity], tokens_ref[...], preferred_element_type=jnp.float32)
            send[step, c] = rows.astype(jnp.bfloat16)

    load_tokens.wait()
    dispatch(0)
    pl.semaphore_wait(barrier, n - 1)

    @pl.loop(0, local)
    def _(step):
        for c in range(CORES):
            forward(step, c).start()
        dispatch(step + 1)

    forward(local, 1 - core).start()
    recv[local, core] = send[local, core]

    logits = lax.dot_general(gate_ref[...], tokens_ref[...], (((1,), (1,)), ((), ())), preferred_element_type=jnp.float32)
    shifted = jnp.exp(logits - jnp.max(logits, axis=0, keepdims=True))
    probs = shifted / jnp.sum(shifted, axis=0, keepdims=True)
    gate_first = jnp.sum(probs * first_hot, axis=0, keepdims=True)
    gate_second = jnp.sum(probs * second_hot, axis=0, keepdims=True)
    gate_total = gate_first + gate_second
    gate_first = gate_first / gate_total
    gate_second = gate_second / gate_total

    load_in.wait()
    load_out.wait()

    def experts_on(step):
        rows = recv[step].reshape(pair, model)
        tile = 512
        for t in range(hid // tile):
            cols = slice(t * tile, (t + 1) * tile)
            up = jnp.dot(rows, w_in[:, cols], preferred_element_type=jnp.float32)
            hidden[:, cols] = jnp.maximum(up, 0.0).astype(jnp.bfloat16)
        tile = 256
        for t in range(model // tile):
            cols = slice(t * tile, (t + 1) * tile)
            down = jnp.dot(hidden[...], w_out[:, cols], preferred_element_type=jnp.float32).astype(jnp.bfloat16)
            for c in range(CORES):
                back[step, c, :, cols] = down[c * capacity:(c + 1) * capacity]

    arrived(local, 1 - core).wait_recv()
    experts_on(local)
    reply(local, 1 - core).start()
    ret[local, core] = back[local, core]

    for step in range(chips):
        base = target_chip(step) * pair
        weight = jnp.where(slot_row == slots[0:1, :] - base, gate_first, 0.0) + jnp.where(slot_row == slots[1:2, :] - base, gate_second, 0.0)
        combine[step] = weight.astype(jnp.bfloat16).T

    @pl.loop(0, local)
    def _(step):
        for c in range(CORES):
            arrived(step, c).wait_recv()
        experts_on(step)
        for c in range(CORES):
            reply(step, c).start()

    block = 256

    def mixed(step, r):
        return jnp.dot(combine[step, r * block:(r + 1) * block, :], ret[step].reshape(pair, model), preferred_element_type=jnp.float32)

    returned(local, 1 - core).wait_recv()
    for r in range(tokens // block):
        total[r * block:(r + 1) * block, :] = mixed(local, r)

    @pl.loop(0, local - 1)
    def _(step):
        for c in range(CORES):
            returned(step, c).wait_recv()
        for r in range(tokens // block):
            total[r * block:(r + 1) * block, :] += mixed(step, r)

    for c in range(CORES):
        returned(local - 1, c).wait_recv()
    for r in range(tokens // block):
        rows = slice(r * block, (r + 1) * block)
        out_ref[rows, :] = (total[rows, :] + mixed(local - 1, r)).astype(jnp.bfloat16)

    @pl.loop(0, local)
    def _(step):
        for c in range(CORES):
            forward(step, c).wait_send()
            reply(step, c).wait_send()

    forward(local, 1 - core).wait_send()
    reply(local, 1 - core).wait_send()


def solution(mesh):
    n = mesh.shape["ep"]
    chips = n // CORES

    def local_layer(tokens, w_gate, expert_ids, keep_second, w_in, w_out):
        count, model = tokens.shape[1:]
        experts = w_gate.shape[1]
        hid = w_in.shape[2]
        capacity = 2 * count // experts
        buffer = pltpu.VMEM((chips, CORES, capacity, model), jnp.bfloat16)
        vmem = pl.BlockSpec(memory_space=pltpu.VMEM)
        hbm = pl.BlockSpec(memory_space=pl.ANY)
        out = pl.pallas_call(
            functools.partial(layer_kernel, n),
            out_shape=jax.ShapeDtypeStruct((count, model), jnp.bfloat16),
            in_specs=[hbm, vmem, vmem, vmem, hbm, hbm],
            out_specs=vmem,
            scratch_shapes=[
                pltpu.VMEM((count, model), jnp.bfloat16),
                pltpu.VMEM((model, hid), jnp.bfloat16),
                pltpu.VMEM((hid, model), jnp.bfloat16),
                buffer, buffer, buffer, buffer,
                pltpu.VMEM((CORES * capacity, hid), jnp.bfloat16),
                pltpu.VMEM((chips, count, CORES * capacity), jnp.bfloat16),
                pltpu.VMEM((count, model), jnp.float32),
                pltpu.VMEM((8, count), jnp.int32),
                pltpu.SemaphoreType.DMA((3,)),
                pltpu.SemaphoreType.DMA((chips, CORES)),
                pltpu.SemaphoreType.DMA((chips, CORES)),
                pltpu.SemaphoreType.DMA((chips, CORES)),
                pltpu.SemaphoreType.DMA((chips, CORES)),
            ],
            compiler_params=pltpu.CompilerParams(collective_id=0, has_side_effects=True, vmem_limit_bytes=58 * 2**20),
        )(tokens[0], w_gate.T, expert_ids[0].T, keep_second, w_in[0], w_out[0])
        return out[None]

    group_spec = P(("dp", "ep"))
    return jax.shard_map(local_layer, mesh=mesh, in_specs=(group_spec, P(), group_spec, group_spec, P("ep"), P("ep")), out_specs=group_spec, check_vma=False)
```

time: 216 us -> 158 us (0.73)
  the two profiles are of different devices: /device:TPU:28 before, /device:TPU:21 now
where the time goes in v1:
time: 158 us
  Pallas kernels  156 us (99%)
  local copies, waits for them, and re-layouts  2.65 us (2%)
    pallas_call x1, Pallas kernels, local_layer(): pl.pallas_call(functools.partial(layer_kernel, n), out_shape=jax.ShapeDty...  156 us

profile of v1, /device:TPU:21, one launch (start us, length us, event | category | flops | bytes accessed | tf_op | source)
XLA Modules:
  0.0 158.3 jit_solution(9929845356009017153)
XLA Ops:
  0.0 155.7 %shard_map.64 = bf16[1024,768]{1,0:T(8,128)(2,1)} custom-call(bf16[1024,768]{1,0:T(8,128)(2,1)} %bitcast.11, bf16[16,768]{1,0:T(8,128)(2,1)} %bitcast.12, s32[2,1024]{1,0:T(2,128)} %bitcast.13, s32[1,1024]{1,0:T(1,128)} %keep_ref.1, bf16[768,3072]{1,0:T(8,128)(2,1)} %bitcast.9, bf16[3072,768]{1,0:T(8,128)(2,1)} %bitcast.10), custom_call_target="tpu_custom_call" | custom-call | tf_op jit(solution)/shard_map/pallas_call | solution.py:227
  155.7 2.7 %copy.8 = bf16[1,1024,768]{2,1,0:T(8,128)(2,1)} copy(bf16[1,1024,768]{2,1,0:T(8,128)(2,1)} %bitcast.8) | data formatting | bytes 3145728

commit v2 on v1

--- a/solution.py
+++ b/solution.py
@@ -49,8 +49,8 @@
     return slot_first, slot_second, first_hot, second_hot
 
 
-def layer_kernel(n, tokens_hbm, gate_ref, ids_ref, keep_ref, w_in_hbm, w_out_hbm, out_ref,
-                 tokens_ref, w_in, w_out, send, recv, back, ret, hidden, combine, total, slots,
+def layer_kernel(n, tokens_hbm, gate_hbm, ids_hbm, keep_hbm, w_in_hbm, w_out_hbm, out_ref,
+                 tokens_ref, gate_ref, ids_ref, keep_ref, w_in, w_out, send, recv, back, ret, hidden, combine, total, slots,
                  load_sem, send_sem, recv_sem, back_sem, ret_sem):
     me = lax.axis_index("ep")
     part = lax.axis_index("dp")
@@ -64,24 +64,37 @@
     pair = CORES * capacity
     local = chips - 1
 
+    load_ids = pltpu.make_async_copy(ids_hbm, ids_ref, load_sem.at[3])
+    load_keep = pltpu.make_async_copy(keep_hbm, keep_ref, load_sem.at[4])
+    load_gate = pltpu.make_async_copy(gate_hbm, gate_ref, load_sem.at[5])
     load_tokens = pltpu.make_async_copy(tokens_hbm, tokens_ref, load_sem.at[0])
     load_in = pltpu.make_async_copy(w_in_hbm, w_in, load_sem.at[1])
     load_out = pltpu.make_async_copy(w_out_hbm, w_out, load_sem.at[2])
+    load_ids.start()
+    load_keep.start()
     load_tokens.start()
-    load_in.start()
-    load_out.start()
+    load_gate.start()
 
     barrier = pltpu.get_barrier_semaphore()
     for k in range(1, n):
         pl.semaphore_signal(barrier, inc=1, device_id=(part, lax.rem(me + k, n)), device_id_type=MESH)
 
+    load_ids.wait()
+    load_keep.wait()
     slot_first, slot_second, first_hot, second_hot = route_slots(ids_ref, keep_ref, experts, capacity)
     slots[0:1, :] = slot_first
     slots[1:2, :] = slot_second
 
+    half = chips // 2
+    order = [half - 1, half + 1, half] + [k for d in range(half - 2, 0, -1) for k in (d, chips - d)] + [0]
+
     def offset_of(step):
-        size = (chips - step) // 2
-        return jnp.where(lax.rem(step, 2) == 1, size, chips - size)
+        if isinstance(step, int):
+            return order[step]
+        offset = order[0]
+        for index, value in enumerate(order[1:-1], 1):
+            offset = jnp.where(step == index, value, offset)
+        return offset
 
     def target_chip(step):
         return lax.rem(chip + offset_of(step), chips)
@@ -119,16 +132,15 @@
         base = target_chip(step) * pair
         hit = (slot_row == slots[0:1, :] - base) | (slot_row == slots[1:2, :] - base)
         pick = jnp.where(hit, 1.0, 0.0).astype(jnp.bfloat16)
-        for c in range(CORES):
-            rows = jnp.dot(pick[c * capacity:(c + 1) * capacity], tokens_ref[...], preferred_element_type=jnp.float32)
-            send[step, c] = rows.astype(jnp.bfloat16)
+        rows = jnp.dot(pick, tokens_ref[...], preferred_element_type=jnp.float32).astype(jnp.bfloat16)
+        send[step] = rows.reshape(CORES, capacity, model)
 
     load_tokens.wait()
+    load_in.start()
+    load_out.start()
     dispatch(0)
     pl.semaphore_wait(barrier, n - 1)
-
-    @pl.loop(0, local)
-    def _(step):
+    for step in range(local):
         for c in range(CORES):
             forward(step, c).start()
         dispatch(step + 1)
@@ -136,6 +148,7 @@
     forward(local, 1 - core).start()
     recv[local, core] = send[local, core]
 
+    load_gate.wait()
     logits = lax.dot_general(gate_ref[...], tokens_ref[...], (((1,), (1,)), ((), ())), preferred_element_type=jnp.float32)
     shifted = jnp.exp(logits - jnp.max(logits, axis=0, keepdims=True))
     probs = shifted / jnp.sum(shifted, axis=0, keepdims=True)
@@ -223,14 +236,17 @@
         capacity = 2 * count // experts
         buffer = pltpu.VMEM((chips, CORES, capacity, model), jnp.bfloat16)
         vmem = pl.BlockSpec(memory_space=pltpu.VMEM)
-        hbm = pl.BlockSpec(memory_space=pl.ANY)
+        hbm = pl.BlockSpec(memory_space=pltpu.HBM)
         out = pl.pallas_call(
             functools.partial(layer_kernel, n),
-            out_shape=jax.ShapeDtypeStruct((count, model), jnp.bfloat16),
-            in_specs=[hbm, vmem, vmem, vmem, hbm, hbm],
+            out_shape=pltpu.VMEM((count, model), jnp.bfloat16),
+            in_specs=[hbm] * 6,
             out_specs=vmem,
             scratch_shapes=[
                 pltpu.VMEM((count, model), jnp.bfloat16),
+                pltpu.VMEM((experts, model), jnp.bfloat16),
+                pltpu.VMEM((2, count), jnp.int32),
+                pltpu.VMEM((1, count), jnp.int32),
                 pltpu.VMEM((model, hid), jnp.bfloat16),
                 pltpu.VMEM((hid, model), jnp.bfloat16),
                 buffer, buffer, buffer, buffer,
@@ -238,14 +254,14 @@
                 pltpu.VMEM((chips, count, CORES * capacity), jnp.bfloat16),
                 pltpu.VMEM((count, model), jnp.float32),
                 pltpu.VMEM((8, count), jnp.int32),
-                pltpu.SemaphoreType.DMA((3,)),
+                pltpu.SemaphoreType.DMA((6,)),
                 pltpu.SemaphoreType.DMA((chips, CORES)),
                 pltpu.SemaphoreType.DMA((chips, CORES)),
                 pltpu.SemaphoreType.DMA((chips, CORES)),
                 pltpu.SemaphoreType.DMA((chips, CORES)),
             ],
-            compiler_params=pltpu.CompilerParams(collective_id=0, has_side_effects=True, vmem_limit_bytes=58 * 2**20),
-        )(tokens[0], w_gate.T, expert_ids[0].T, keep_second, w_in[0], w_out[0])
+            compiler_params=pltpu.CompilerParams(collective_id=0, has_side_effects=True, vmem_limit_bytes=50 * 2**20),
+        )(*(pltpu.with_memory_space_constraint(x, pltpu.HBM) for x in (tokens[0], w_gate.T, expert_ids[0].T, keep_second, w_in[0], w_out[0])))
         return out[None]
 
     group_spec = P(("dp", "ep"))

time: 158 us -> 150 us (0.949)
  Pallas kernels: 156 us -> 149 us
    pallas_call x1, Pallas kernels: 156 us -> 149 us  [local_layer(): pl.pallas_call(functools.partial(layer_kernel, n), out_shape=pltpu.VMEM((...]
where the time goes in v2:
time: 150 us
  Pallas kernels  149 us (99%)
    pallas_call x1, Pallas kernels, local_layer(): pl.pallas_call(functools.partial(layer_kernel, n), out_shape=pltpu.VMEM((...  149 us

profile of v2, /device:TPU:21, one launch (start us, length us, event | category | flops | bytes accessed | tf_op | source)
XLA Modules:
  0.0 150.3 jit_solution(14486066868846136382)
XLA Ops:
  0.0 149.1 %shard_map.64 = bf16[1024,768]{1,0:T(8,128)(2,1)S(1)} custom-call(bf16[1024,768]{1,0:T(8,128)(2,1)} %bitcast.11, bf16[16,768]{1,0:T(8,128)(2,1)} %bitcast.12, s32[2,1024]{1,0:T(2,128)} %bitcast.13, s32[1,1024]{1,0:T(1,128)} %keep_hbm.1, bf16[768,3072]{1,0:T(8,128)(2,1)} %bitcast.9, bf16[3072,768]{1,0:T(8,128)(2,1)} %bitcast.10), custom_call_target="tpu_custom_call" | custom-call | tf_op jit(solution)/shard_map/pallas_call | solution.py:240
  149.2 1.1 copy.8

commit v3 on v2

--- a/solution.py
+++ b/solution.py
@@ -50,7 +50,7 @@
 
 
 def layer_kernel(n, tokens_hbm, gate_hbm, ids_hbm, keep_hbm, w_in_hbm, w_out_hbm, out_ref,
-                 tokens_ref, gate_ref, ids_ref, keep_ref, w_in, w_out, send, recv, back, ret, hidden, combine, total, slots,
+                 tokens_ref, gate_ref, ids_ref, keep_ref, w_in, w_out, send, recv, back, ret, hidden, combine, total, slots, picks,
                  load_sem, send_sem, recv_sem, back_sem, ret_sem):
     me = lax.axis_index("ep")
     part = lax.axis_index("dp")
@@ -67,12 +67,15 @@
     load_ids = pltpu.make_async_copy(ids_hbm, ids_ref, load_sem.at[3])
     load_keep = pltpu.make_async_copy(keep_hbm, keep_ref, load_sem.at[4])
     load_gate = pltpu.make_async_copy(gate_hbm, gate_ref, load_sem.at[5])
-    load_tokens = pltpu.make_async_copy(tokens_hbm, tokens_ref, load_sem.at[0])
-    load_in = pltpu.make_async_copy(w_in_hbm, w_in, load_sem.at[1])
-    load_out = pltpu.make_async_copy(w_out_hbm, w_out, load_sem.at[2])
+    quarter = tokens // 4
+    quarters = [slice(k * quarter, (k + 1) * quarter) for k in range(4)]
+    load_tokens = [pltpu.make_async_copy(tokens_hbm.at[rows], tokens_ref.at[rows], load_sem.at[6 + k]) for k, rows in enumerate(quarters)]
+    load_in = pltpu.make_async_copy(w_in_hbm, w_in, load_sem.at[0])
+    load_out = pltpu.make_async_copy(w_out_hbm, w_out, load_sem.at[1])
     load_ids.start()
     load_keep.start()
-    load_tokens.start()
+    for load in load_tokens:
+        load.start()
     load_gate.start()
 
     barrier = pltpu.get_barrier_semaphore()
@@ -86,7 +89,7 @@
     slots[1:2, :] = slot_second
 
     half = chips // 2
-    order = [half - 1, half + 1, half] + [k for d in range(half - 2, 0, -1) for k in (d, chips - d)] + [0]
+    order = [k for d in range(half - 1, 1, -1) for k in (d, chips - d)] + [half, 1, chips - 1, 0]
 
     def offset_of(step):
         if isinstance(step, int):
@@ -128,22 +131,48 @@
 
     slot_row = lax.broadcasted_iota(jnp.int32, (pair, tokens), 0)
 
-    def dispatch(step):
+    def pick_of(step):
         base = target_chip(step) * pair
         hit = (slot_row == slots[0:1, :] - base) | (slot_row == slots[1:2, :] - base)
-        pick = jnp.where(hit, 1.0, 0.0).astype(jnp.bfloat16)
-        rows = jnp.dot(pick, tokens_ref[...], preferred_element_type=jnp.float32).astype(jnp.bfloat16)
-        send[step] = rows.reshape(CORES, capacity, model)
-
-    load_tokens.wait()
+        return jnp.where(hit, 1.0, 0.0).astype(jnp.bfloat16)
+
+    def keep_rows(step, rows):
+        send[step] = rows.astype(jnp.bfloat16).reshape(CORES, capacity, model)
+
+    def start_forward(step):
+        for c in (core, 1 - core):
+            forward(step, c).start()
+
+    def turn(index):
+        mirror = order.index((chips - order[index]) % chips)
+        return index
+
+    early = (turn(0), turn(1))
+    for k, step in enumerate(early):
+        picks[k] = pick_of(step)
+    for load, rows in zip(load_tokens[:-1], quarters[:-1]):
+        load.wait()
+        for k in range(2):
+            part_sum = jnp.dot(picks[k, :, rows], tokens_ref[rows, :], preferred_element_type=jnp.float32)
+            kept = slice(k * pair, (k + 1) * pair)
+            if rows.start == 0:
+                total[kept, :] = part_sum
+            else:
+                total[kept, :] += part_sum
+    load_tokens[-1].wait()
     load_in.start()
     load_out.start()
-    dispatch(0)
-    pl.semaphore_wait(barrier, n - 1)
-    for step in range(local):
-        for c in range(CORES):
-            forward(step, c).start()
-        dispatch(step + 1)
+    for k, step in enumerate(early):
+        rows = quarters[-1]
+        keep_rows(step, total[k * pair:(k + 1) * pair, :] + jnp.dot(picks[k, :, rows], tokens_ref[rows, :], preferred_element_type=jnp.float32))
+        if k == 0:
+            pl.semaphore_wait(barrier, n - 1)
+        start_forward(step)
+    for index in range(2, chips):
+        step = turn(index)
+        keep_rows(step, jnp.dot(pick_of(step), tokens_ref[...], preferred_element_type=jnp.float32))
+        if index < local:
+            start_forward(step)
 
     forward(local, 1 - core).start()
     recv[local, core] = send[local, core]
@@ -190,7 +219,7 @@
         for c in range(CORES):
             arrived(step, c).wait_recv()
         experts_on(step)
-        for c in range(CORES):
+        for c in (1, 0):
             reply(step, c).start()
 
     block = 256
@@ -254,7 +283,8 @@
                 pltpu.VMEM((chips, count, CORES * capacity), jnp.bfloat16),
                 pltpu.VMEM((count, model), jnp.float32),
                 pltpu.VMEM((8, count), jnp.int32),
-                pltpu.SemaphoreType.DMA((6,)),
+                pltpu.VMEM((2, CORES * capacity, count), jnp.bfloat16),
+                pltpu.SemaphoreType.DMA((10,)),
                 pltpu.SemaphoreType.DMA((chips, CORES)),
                 pltpu.SemaphoreType.DMA((chips, CORES)),
                 pltpu.SemaphoreType.DMA((chips, CORES)),

time: 150 us -> 149 us (level)
  the two profiles are of different devices: /device:TPU:21 before, /device:TPU:28 now
where the time goes in v3:
time: 149 us
  Pallas kernels  148 us (99%)
    pallas_call x1, Pallas kernels, local_layer(): pl.pallas_call(functools.partial(layer_kernel, n), out_shape=pltpu.VMEM((...  148 us

profile of v3, /device:TPU:28, one launch (start us, length us, event | category | flops | bytes accessed | tf_op | source)
XLA Modules:
  0.0 149.1 jit_solution(11884096972548290923)
XLA Ops:
  0.0 148.0 %shard_map.64 = bf16[1024,768]{1,0:T(8,128)(2,1)S(1)} custom-call(bf16[1024,768]{1,0:T(8,128)(2,1)} %bitcast.11, bf16[16,768]{1,0:T(8,128)(2,1)} %bitcast.12, s32[2,1024]{1,0:T(2,128)} %bitcast.13, s32[1,1024]{1,0:T(1,128)} %keep_hbm.1, bf16[768,3072]{1,0:T(8,128)(2,1)} %bitcast.9, bf16[3072,768]{1,0:T(8,128)(2,1)} %bitcast.10), custom_call_target="tpu_custom_call" | custom-call | tf_op jit(solution)/shard_map/pallas_call | solution.py:269
  148.0 1.1 copy.8

commit v4 on v2

v4 whole, which is shorter than its diff:
```python
import functools
import math

import jax
import jax.numpy as jnp
from jax import lax
from jax.experimental import pallas as pl
from jax.experimental.pallas import tpu as pltpu
from jax.sharding import PartitionSpec as P

MESH = pl.DeviceIdType.MESH
CORES = 2
LANES = 128


def route_slots(ids_ref, keep_ref, experts, capacity):
    tokens = ids_ref.shape[1]
    first = ids_ref[0:1, :]
    second = ids_ref[1:2, :]
    keep = keep_ref[0:1, :]
    expert_row = lax.broadcasted_iota(jnp.int32, (experts, tokens), 0)
    first_hot = jnp.where(expert_row == first, 1.0, 0.0)
    second_hot = jnp.where((expert_row == second) & (keep == 1), 1.0, 0.0)
    hot = jnp.concatenate([first_hot, second_hot], axis=0)
    blocks = tokens // LANES
    stacked = jnp.concatenate([hot[:, b * LANES:(b + 1) * LANES] for b in range(blocks)], axis=0).astype(jnp.bfloat16)
    row = lax.broadcasted_iota(jnp.int32, (LANES, 2 * LANES), 0)
    col = lax.broadcasted_iota(jnp.int32, (LANES, 2 * LANES), 1)
    before = jnp.where((row < col) | (col >= LANES), 1.0, 0.0).astype(jnp.bfloat16)
    counts = jnp.dot(stacked, before, preferred_element_type=jnp.float32)
    rows = 2 * experts
    offset = jnp.zeros((rows, LANES), jnp.float32)
    prefix = []
    for b in range(blocks):
        part = counts[b * rows:(b + 1) * rows]
        prefix.append(part[:, :LANES] + offset)
        offset = offset + part[:, LANES:]
    first_total = offset[:experts]
    slot_first, slot_second = [], []
    for b in range(blocks):
        lanes = slice(b * LANES, (b + 1) * LANES)
        pos_first = jnp.sum(prefix[b][:experts] * first_hot[:, lanes], axis=0, keepdims=True)
        pos_second = jnp.sum((prefix[b][experts:] + first_total) * second_hot[:, lanes], axis=0, keepdims=True)
        slot_first.append(pos_first)
        slot_second.append(pos_second)
    pos_first = jnp.concatenate(slot_first, axis=1).astype(jnp.int32)
    pos_second = jnp.concatenate(slot_second, axis=1).astype(jnp.int32)
    slot_first = jnp.where(pos_first < capacity, first * capacity + pos_first, -1)
    slot_second = jnp.where((keep == 1) & (pos_second < capacity), second * capacity + pos_second, -1)
    return slot_first, slot_second, first_hot, second_hot


def layer_kernel(n, groups, tokens_hbm, gate_hbm, ids_hbm, keep_hbm, w_in_hbm, w_out_hbm, out_ref,
                 tokens_ref, gate_ref, ids_ref, keep_ref, w_in, w_out, host_in, host_out, send, recv, back, ret, hidden, combine, total, slots,
                 load_sem, send_sem, recv_sem, back_sem, ret_sem, lend_sem, share_sem, slice_sem):
    me = lax.axis_index("ep")
    part = lax.axis_index("dp")
    chips = n // CORES
    half = chips // 2
    chip = me // CORES
    core = lax.rem(me, CORES)
    side = 1 - 2 * core
    experts = gate_ref.shape[0]
    tokens, model = tokens_ref.shape
    hid = w_in.shape[1]
    capacity = 2 * tokens // experts
    pair = CORES * capacity
    span = math.isqrt(groups)
    part_x = part // span
    part_y = lax.rem(part, span)

    load_ids = pltpu.make_async_copy(ids_hbm, ids_ref, load_sem.at[0])
    load_keep = pltpu.make_async_copy(keep_hbm, keep_ref, load_sem.at[1])
    load_gate = pltpu.make_async_copy(gate_hbm, gate_ref, load_sem.at[2])
    load_tokens = pltpu.make_async_copy(tokens_hbm, tokens_ref, load_sem.at[3])
    load_in = pltpu.make_async_copy(w_in_hbm, w_in, load_sem.at[4])
    load_out = pltpu.make_async_copy(w_out_hbm, w_out, load_sem.at[5])
    load_ids.start()
    load_keep.start()
    load_tokens.start()
    load_gate.start()

    def share_peer(array, phase, shift):
        if (array == 0) == (phase == 0):
            return lax.rem(part_x + shift, span) * span + part_y
        return part_x * span + lax.rem(part_y + shift, span)

    barrier = pltpu.get_barrier_semaphore()
    for k in range(1, n):
        pl.semaphore_signal(barrier, inc=1, device_id=(part, lax.rem(me + k, n)), device_id_type=MESH)
    for phase in range(2):
        for shift in range(1, span):
            pl.semaphore_signal(barrier, inc=1, device_id=(share_peer(0, phase, shift), me), device_id_type=MESH)

    load_ids.wait()
    load_keep.wait()
    slot_first, slot_second, first_hot, second_hot = route_slots(ids_ref, keep_ref, experts, capacity)
    slots[0:1, :] = slot_first
    slots[1:2, :] = slot_second

    def wrap(value):
        return lax.rem(value + chips, chips)

    def run_chip(hosted, j, c):
        sign = 1 - 2 * c
        return wrap(chip + sign * j) if hosted else wrap(chip - sign * j)

    def expert_of(hosted, j, c):
        sign = 1 - 2 * c
        return (wrap(run_chip(hosted, j, c) + sign) if hosted else run_chip(hosted, j, c)) * CORES + c

    def source_chip(hosted, j):
        return wrap(chip - side * j) if hosted else wrap(chip + side * j)

    def forward(hosted, j, c):
        step = hosted * half + j
        return pltpu.make_async_remote_copy(
            src_ref=send.at[step, c], dst_ref=recv.at[step, core],
            send_sem=send_sem.at[step, c], recv_sem=recv_sem.at[step, core],
            device_id=(part, run_chip(hosted, j, c) * CORES + c), device_id_type=MESH)

    def arrived(hosted, j, c):
        step = hosted * half + j
        return pltpu.make_async_remote_copy(
            src_ref=send.at[step, c], dst_ref=recv.at[step, c],
            send_sem=send_sem.at[step, c], recv_sem=recv_sem.at[step, c],
            device_id=(part, run_chip(hosted, j, c) * CORES + c), device_id_type=MESH)

    def reply(hosted, j, c):
        step = hosted * half + j
        return pltpu.make_async_remote_copy(
            src_ref=back.at[step, c], dst_ref=ret.at[step, core],
            send_sem=back_sem.at[step, c], recv_sem=ret_sem.at[step, core],
            device_id=(part, source_chip(hosted, j) * CORES + c), device_id_type=MESH)

    def returned(hosted, j, c):
        step = hosted * half + j
        return pltpu.make_async_remote_copy(
            src_ref=back.at[step, c], dst_ref=ret.at[step, c],
            send_sem=back_sem.at[step, c], recv_sem=ret_sem.at[step, c],
            device_id=(part, source_chip(hosted, j) * CORES + c), device_id_type=MESH)

    own_hbm = (w_in_hbm, w_out_hbm)
    host = (host_in, host_out)

    def slice_of(array, owner):
        rows = host[array].shape[0] // groups
        return pl.ds(pl.multiple_of(owner * rows, rows), rows)

    def lend(array):
        return pltpu.make_async_remote_copy(
            src_ref=own_hbm[array].at[slice_of(array, part)], dst_ref=host[array].at[slice_of(array, part)],
            send_sem=lend_sem.at[array], recv_sem=slice_sem.at[array, part],
            device_id=(part, wrap(chip - side) * CORES + core), device_id_type=MESH)

    def slice_owner(array, shift):
        return share_peer(array, 0, shift)

    def share(array, phase, k, shift):
        owner = slice_owner(array, k)
        return pltpu.make_async_remote_copy(
            src_ref=host[array].at[slice_of(array, owner)], dst_ref=host[array].at[slice_of(array, owner)],
            send_sem=share_sem.at[array, phase, k, shift], recv_sem=slice_sem.at[array, owner],
            device_id=(share_peer(array, phase, shift), me), device_id_type=MESH)

    def slice_ready(array, owner):
        return pltpu.make_async_remote_copy(
            src_ref=host[array].at[slice_of(array, owner)], dst_ref=host[array].at[slice_of(array, owner)],
            send_sem=lend_sem.at[array], recv_sem=slice_sem.at[array, owner],
            device_id=(share_peer(0, 0, 1), me), device_id_type=MESH)

    slot_row = lax.broadcasted_iota(jnp.int32, (capacity, tokens), 0)

    def pick_of(hosted, j):
        halves = []
        for c in range(CORES):
            base = expert_of(hosted, j, c) * capacity
            hit = (slot_row == slots[0:1, :] - base) | (slot_row == slots[1:2, :] - base)
            halves.append(jnp.where(hit, 1.0, 0.0))
        return jnp.concatenate(halves, axis=0).astype(jnp.bfloat16)

    def dispatch(hosted, j):
        rows = jnp.dot(pick_of(hosted, j), tokens_ref[...], preferred_element_type=jnp.float32).astype(jnp.bfloat16)
        send[hosted * half + j] = rows.reshape(CORES, capacity, model)

    load_tokens.wait()
    load_in.start()
    load_out.start()
    pl.semaphore_wait(barrier, n - 1 + 2 * (span - 1))
    lend(0).start()
    lend(1).start()
    far_first = range(half - 1, 0, -1)
    for hosted in range(2):
        for j in (*far_first, 0):
            dispatch(hosted, j)
    for hosted in range(2):
        forward(hosted, 0, 1 - core).start()
        recv[hosted * half, core] = send[hosted * half, core]

    load_gate.wait()
    logits = lax.dot_general(gate_ref[...], tokens_ref[...], (((1,), (1,)), ((), ())), preferred_element_type=jnp.float32)
    shifted = jnp.exp(logits - jnp.max(logits, axis=0, keepdims=True))
    probs = shifted / jnp.sum(shifted, axis=0, keepdims=True)
    gate_first = jnp.sum(probs * first_hot, axis=0, keepdims=True)
    gate_second = jnp.sum(probs * second_hot, axis=0, keepdims=True)
    gate_total = gate_first + gate_second
    gate_first = gate_first / gate_total
    gate_second = gate_second / gate_total
    for hosted in range(2):
        for j in range(half):
            weights = []
            for c in range(CORES):
                base = expert_of(hosted, j, c) * capacity
                weights.append(jnp.where(slot_row == slots[0:1, :] - base, gate_first, 0.0) + jnp.where(slot_row == slots[1:2, :] - base, gate_second, 0.0))
            combine[hosted * half + j] = jnp.concatenate(weights, axis=0).astype(jnp.bfloat16).T

    load_in.wait()
    load_out.wait()

    def experts_on(hosted, j):
        step = hosted * half + j
        up_ref, down_ref = (host_in, host_out) if hosted else (w_in, w_out)
        rows = recv[step].reshape(pair, model)
        tile = 512
        for t in range(hid // tile):
            cols = slice(t * tile, (t + 1) * tile)
            up = jnp.dot(rows, up_ref[:, cols], preferred_element_type=jnp.float32)
            hidden[:, cols] = jnp.maximum(up, 0.0).astype(jnp.bfloat16)
        tile = 256
        for t in range(model // tile):
            cols = slice(t * tile, (t + 1) * tile)
            down = jnp.dot(hidden[...], down_ref[:, cols], preferred_element_type=jnp.float32).astype(jnp.bfloat16)
            for c in range(CORES):
                back[step, c, :, cols] = down[c * capacity:(c + 1) * capacity]

    def local_experts(hosted):
        arrived(hosted, 0, 1 - core).wait_recv()
        experts_on(hosted, 0)
        reply(hosted, 0, 1 - core).start()
        ret[hosted * half, core] = back[hosted * half, core]

    def remote_experts(hosted):
        @pl.loop(0, half - 1)
        def _(index):
            j = half - 1 - index
            for c in range(CORES):
                arrived(hosted, j, c).wait_recv()
            experts_on(hosted, j)
            for c in (1, 0):
                reply(hosted, j, c).start()

    def first_share(array):
        slice_ready(array, part).wait_recv()
        for shift in range(1, span):
            share(array, 0, 0, shift).start()
        for shift in range(1, span):
            share(array, 1, 0, shift).start()

    def second_share(array):
        for k in range(1, span):
            slice_ready(array, slice_owner(array, k)).wait_recv()
            for shift in range(1, span):
                share(array, 1, k, shift).start()

    first_share(0)
    local_experts(0)
    for hosted in range(2):
        for j in far_first:
            for c in (core, 1 - core):
                forward(hosted, j, c).start()
    first_share(1)
    second_share(0)
    remote_experts(0)
    second_share(1)
    for array in range(2):
        for k in range(span):
            for shift in range(1, span):
                owner = share_peer(0, 0, k) // span * span + lax.rem(part_y + shift, span) if array == 0 else lax.rem(part_x + shift, span) * span + lax.rem(part_y + k, span)
                slice_ready(array, owner).wait_recv()
    local_experts(1)
    remote_experts(1)

    block = 256

    def mixed(step, r):
        return jnp.dot(combine[step, r * block:(r + 1) * block, :], ret[step].reshape(pair, model), preferred_element_type=jnp.float32)

    for hosted in range(2):
        returned(hosted, 0, 1 - core).wait_recv()
        for r in range(tokens // block):
            rows = slice(r * block, (r + 1) * block)
            if hosted == 0:
                total[rows, :] = mixed(0, r)
            else:
                total[rows, :] += mixed(half, r)
        count = half - 1 if hosted == 0 else half - 2

        @pl.loop(0, count)
        def _(index):
            j = half - 1 - index
            for c in range(CORES):
                returned(hosted, j, c).wait_recv()
            for r in range(tokens // block):
                total[r * block:(r + 1) * block, :] += mixed(hosted * half + j, r)

    for c in range(CORES):
        returned(1, 1, c).wait_recv()
    for r in range(tokens // block):
        rows = slice(r * block, (r + 1) * block)
        out_ref[rows, :] = (total[rows, :] + mixed(half + 1, r)).astype(jnp.bfloat16)

    for hosted in range(2):
        forward(hosted, 0, 1 - core).wait_send()
        reply(hosted, 0, 1 - core).wait_send()

        @pl.loop(1, half)
        def _(j):
            for c in range(CORES):
                forward(hosted, j, c).wait_send()
                reply(hosted, j, c).wait_send()
    for array in range(2):
        lend(array).wait_send()
        for phase in range(2):
            for k in range(span if phase == 1 else 1):
                for shift in range(1, span):
                    share(array, phase, k, shift).wait_send()


def solution(mesh):
    n = mesh.shape["ep"]
    chips = n // CORES
    groups = mesh.shape["dp"]
    span = math.isqrt(groups)

    def local_layer(tokens, w_gate, expert_ids, keep_second, w_in, w_out):
        count, model = tokens.shape[1:]
        experts = w_gate.shape[1]
        hid = w_in.shape[2]
        capacity = 2 * count // experts
        buffer = pltpu.VMEM((chips, CORES, capacity, model), jnp.bfloat16)
        vmem = pl.BlockSpec(memory_space=pltpu.VMEM)
        hbm = pl.BlockSpec(memory_space=pltpu.HBM)
        out = pl.pallas_call(
            functools.partial(layer_kernel, n, groups),
            out_shape=pltpu.VMEM((count, model), jnp.bfloat16),
            in_specs=[hbm] * 6,
            out_specs=vmem,
            scratch_shapes=[
                pltpu.VMEM((count, model), jnp.bfloat16),
                pltpu.VMEM((experts, model), jnp.bfloat16),
                pltpu.VMEM((2, count), jnp.int32),
                pltpu.VMEM((1, count), jnp.int32),
                pltpu.VMEM((model, hid), jnp.bfloat16),
                pltpu.VMEM((hid, model), jnp.bfloat16),
                pltpu.VMEM((model, hid), jnp.bfloat16),
                pltpu.VMEM((hid, model), jnp.bfloat16),
                buffer, buffer, buffer, buffer,
                pltpu.VMEM((CORES * capacity, hid), jnp.bfloat16),
                pltpu.VMEM((chips, count, CORES * capacity), jnp.bfloat16),
                pltpu.VMEM((count, model), jnp.float32),
                pltpu.VMEM((8, count), jnp.int32),
                pltpu.SemaphoreType.DMA((6,)),
                pltpu.SemaphoreType.DMA((chips, CORES)),
                pltpu.SemaphoreType.DMA((chips, CORES)),
                pltpu.SemaphoreType.DMA((chips, CORES)),
                pltpu.SemaphoreType.DMA((chips, CORES)),
                pltpu.SemaphoreType.DMA((2,)),
                pltpu.SemaphoreType.DMA((2, 2, span, span)),
                pltpu.SemaphoreType.DMA((2, groups)),
            ],
            compiler_params=pltpu.CompilerParams(collective_id=0, has_side_effects=True, vmem_limit_bytes=54 * 2**20),
        )(*(pltpu.with_memory_space_constraint(x, pltpu.HBM) for x in (tokens[0], w_gate.T, expert_ids[0].T, keep_second, w_in[0], w_out[0])))
        return out[None]

    group_spec = P(("dp", "ep"))
    return jax.shard_map(local_layer, mesh=mesh, in_specs=(group_spec, P(), group_spec, group_spec, P("ep"), P("ep")), out_specs=group_spec, check_vma=False)
```

time: 150 us -> 142 us (0.947)
  the two profiles are of different devices: /device:TPU:21 before, /device:TPU:28 now
where the time goes in v4:
time: 142 us
  Pallas kernels  141 us (99%)
    pallas_call x1, Pallas kernels, local_layer(): pl.pallas_call(functools.partial(layer_kernel, n, groups), out_shape=pltp...  141 us

profile of v4, /device:TPU:28, one launch (start us, length us, event | category | flops | bytes accessed | tf_op | source)
XLA Modules:
  0.0 141.9 jit_solution(4092815598659686641)
XLA Ops:
  0.0 140.8 %shard_map.64 = bf16[1024,768]{1,0:T(8,128)(2,1)S(1)} custom-call(bf16[1024,768]{1,0:T(8,128)(2,1)} %bitcast.11, bf16[16,768]{1,0:T(8,128)(2,1)} %bitcast.12, s32[2,1024]{1,0:T(2,128)} %bitcast.13, s32[1,1024]{1,0:T(1,128)} %keep_hbm.1, bf16[768,3072]{1,0:T(8,128)(2,1)} %bitcast.9, bf16[3072,768]{1,0:T(8,128)(2,1)} %bitcast.10), custom_call_target="tpu_custom_call" | custom-call | tf_op jit(solution)/shard_map/pallas_call | solution.py:343
  140.8 1.1 copy.8

commit v5 on v4

--- a/solution.py
+++ b/solution.py
@@ -52,7 +52,7 @@
 
 def layer_kernel(n, groups, tokens_hbm, gate_hbm, ids_hbm, keep_hbm, w_in_hbm, w_out_hbm, out_ref,
                  tokens_ref, gate_ref, ids_ref, keep_ref, w_in, w_out, host_in, host_out, send, recv, back, ret, hidden, combine, total, slots,
-                 load_sem, send_sem, recv_sem, back_sem, ret_sem, lend_sem, share_sem, slice_sem):
+                 load_sem, send_sem, recv_sem, back_sem, ret_sem, lend_sem, share_sem, slice_sem, reach_sem):
     me = lax.axis_index("ep")
     part = lax.axis_index("dp")
     chips = n // CORES
@@ -86,72 +86,84 @@
         return part_x * span + lax.rem(part_y + shift, span)
 
     barrier = pltpu.get_barrier_semaphore()
-    for k in range(1, n):
-        pl.semaphore_signal(barrier, inc=1, device_id=(part, lax.rem(me + k, n)), device_id_type=MESH)
+    ahead, behind, partner = lax.rem(me + CORES, n), lax.rem(me + n - CORES, n), me + 1 - 2 * core
+    for near in (ahead, behind, partner):
+        pl.semaphore_signal(barrier, inc=1, device_id=(part, near), device_id_type=MESH)
     for phase in range(2):
         for shift in range(1, span):
             pl.semaphore_signal(barrier, inc=1, device_id=(share_peer(0, phase, shift), me), device_id_type=MESH)
+
+
+    def wrap(value):
+        return lax.rem(value + chips, chips)
+
+    def run_chip(hosted, j, c):
+        sign = 1 - 2 * c
+        return wrap(chip + sign * j) if hosted else wrap(chip - sign * j)
+
+    def expert_of(hosted, j, c):
+        sign = 1 - 2 * c
+        return (wrap(run_chip(hosted, j, c) + sign) if hosted else run_chip(hosted, j, c)) * CORES + c
+
+    def source_chip(hosted, j):
+        return wrap(chip - side * j) if hosted else wrap(chip + side * j)
+
+    def forward(hosted, j, c):
+        step = hosted * half + j
+        return pltpu.make_async_remote_copy(
+            src_ref=send.at[step, c], dst_ref=recv.at[step, core],
+            send_sem=send_sem.at[step, c], recv_sem=recv_sem.at[step, core],
+            device_id=(part, run_chip(hosted, j, c) * CORES + c), device_id_type=MESH)
+
+    def arrived(hosted, j, c):
+        step = hosted * half + j
+        return pltpu.make_async_remote_copy(
+            src_ref=send.at[step, c], dst_ref=recv.at[step, c],
+            send_sem=send_sem.at[step, c], recv_sem=recv_sem.at[step, c],
+            device_id=(part, run_chip(hosted, j, c) * CORES + c), device_id_type=MESH)
+
+    def reply(hosted, j, c):
+        step = hosted * half + j
+        return pltpu.make_async_remote_copy(
+            src_ref=back.at[step, c], dst_ref=ret.at[step, core],
+            send_sem=back_sem.at[step, c], recv_sem=ret_sem.at[step, core],
+            device_id=(part, source_chip(hosted, j) * CORES + c), device_id_type=MESH)
+
+    def returned(hosted, j, c):
+        step = hosted * half + j
+        return pltpu.make_async_remote_copy(
+            src_ref=back.at[step, c], dst_ref=ret.at[step, c],
+            send_sem=back_sem.at[step, c], recv_sem=ret_sem.at[step, c],
+            device_id=(part, source_chip(hosted, j) * CORES + c), device_id_type=MESH)
+
+    own_hbm = (w_in_hbm, w_out_hbm)
+    host = (host_in, host_out)
+
+    def slice_of(array, owner):
+        rows = host[array].shape[0] // groups
+        return pl.ds(pl.multiple_of(owner * rows, rows), rows)
+
+    def lend(array):
+        return pltpu.make_async_remote_copy(
+            src_ref=own_hbm[array].at[slice_of(array, part)], dst_ref=host[array].at[slice_of(array, part)],
+            send_sem=lend_sem.at[array], recv_sem=slice_sem.at[array, part],
+            device_id=(part, wrap(chip - side) * CORES + core), device_id_type=MESH)
+
+    pl.semaphore_wait(barrier, 3 + 2 * (span - 1))
+    lend(0).start()
+    lend(1).start()
+    for level in range(half - 1):
+        for near in (ahead, behind):
+            pl.semaphore_signal(reach_sem.at[level], inc=1, device_id=(part, near), device_id_type=MESH)
+        pl.semaphore_wait(reach_sem.at[level], 2)
+    pl.semaphore_signal(reach_sem.at[half - 1], inc=1, device_id=(part, partner), device_id_type=MESH)
+    pl.semaphore_wait(reach_sem.at[half - 1], 1)
 
     load_ids.wait()
     load_keep.wait()
     slot_first, slot_second, first_hot, second_hot = route_slots(ids_ref, keep_ref, experts, capacity)
     slots[0:1, :] = slot_first
     slots[1:2, :] = slot_second
-
-    def wrap(value):
-        return lax.rem(value + chips, chips)
-
-    def run_chip(hosted, j, c):
-        sign = 1 - 2 * c
-        return wrap(chip + sign * j) if hosted else wrap(chip - sign * j)
-
-    def expert_of(hosted, j, c):
-        sign = 1 - 2 * c
-        return (wrap(run_chip(hosted, j, c) + sign) if hosted else run_chip(hosted, j, c)) * CORES + c
-
-    def source_chip(hosted, j):
-        return wrap(chip - side * j) if hosted else wrap(chip + side * j)
-
-    def forward(hosted, j, c):
-        step = hosted * half + j
-        return pltpu.make_async_remote_copy(
-            src_ref=send.at[step, c], dst_ref=recv.at[step, core],
-            send_sem=send_sem.at[step, c], recv_sem=recv_sem.at[step, core],
-            device_id=(part, run_chip(hosted, j, c) * CORES + c), device_id_type=MESH)
-
-    def arrived(hosted, j, c):
-        step = hosted * half + j
-        return pltpu.make_async_remote_copy(
-            src_ref=send.at[step, c], dst_ref=recv.at[step, c],
-            send_sem=send_sem.at[step, c], recv_sem=recv_sem.at[step, c],
-            device_id=(part, run_chip(hosted, j, c) * CORES + c), device_id_type=MESH)
-
-    def reply(hosted, j, c):
-        step = hosted * half + j
-        return pltpu.make_async_remote_copy(
-            src_ref=back.at[step, c], dst_ref=ret.at[step, core],
-            send_sem=back_sem.at[step, c], recv_sem=ret_sem.at[step, core],
-            device_id=(part, source_chip(hosted, j) * CORES + c), device_id_type=MESH)
-
-    def returned(hosted, j, c):
-        step = hosted * half + j
-        return pltpu.make_async_remote_copy(
-            src_ref=back.at[step, c], dst_ref=ret.at[step, c],
-            send_sem=back_sem.at[step, c], recv_sem=ret_sem.at[step, c],
-            device_id=(part, source_chip(hosted, j) * CORES + c), device_id_type=MESH)
-
-    own_hbm = (w_in_hbm, w_out_hbm)
-    host = (host_in, host_out)
-
-    def slice_of(array, owner):
-        rows = host[array].shape[0] // groups
-        return pl.ds(pl.multiple_of(owner * rows, rows), rows)
-
-    def lend(array):
-        return pltpu.make_async_remote_copy(
-            src_ref=own_hbm[array].at[slice_of(array, part)], dst_ref=host[array].at[slice_of(array, part)],
-            send_sem=lend_sem.at[array], recv_sem=slice_sem.at[array, part],
-            device_id=(part, wrap(chip - side) * CORES + core), device_id_type=MESH)
 
     def slice_owner(array, shift):
         return share_peer(array, 0, shift)
@@ -186,9 +198,6 @@
     load_tokens.wait()
     load_in.start()
     load_out.start()
-    pl.semaphore_wait(barrier, n - 1 + 2 * (span - 1))
-    lend(0).start()
-    lend(1).start()
     far_first = range(half - 1, 0, -1)
     for hosted in range(2):
         for j in (*far_first, 0):
@@ -277,8 +286,8 @@
             for shift in range(1, span):
                 owner = share_peer(0, 0, k) // span * span + lax.rem(part_y + shift, span) if array == 0 else lax.rem(part_x + shift, span) * span + lax.rem(part_y + k, span)
                 slice_ready(array, owner).wait_recv()
+    remote_experts(1)
     local_experts(1)
-    remote_experts(1)
 
     block = 256
 
@@ -367,6 +376,7 @@
                 pltpu.SemaphoreType.DMA((2,)),
                 pltpu.SemaphoreType.DMA((2, 2, span, span)),
                 pltpu.SemaphoreType.DMA((2, groups)),
+                pltpu.SemaphoreType.REGULAR((chips // 2,)),
             ],
             compiler_params=pltpu.CompilerParams(collective_id=0, has_side_effects=True, vmem_limit_bytes=54 * 2**20),
         )(*(pltpu.with_memory_space_constraint(x, pltpu.HBM) for x in (tokens[0], w_gate.T, expert_ids[0].T, keep_second, w_in[0], w_out[0])))

time: 142 us -> 141 us (level)
  no operation moved by 1% of the time
where the time goes in v5:
time: 141 us
  Pallas kernels  140 us (99%)
    pallas_call x1, Pallas kernels, local_layer(): pl.pallas_call(functools.partial(layer_kernel, n, groups), out_shape=pltp...  140 us

profile of v5, /device:TPU:28, one launch (start us, length us, event | category | flops | bytes accessed | tf_op | source)
XLA Modules:
  0.0 140.9 jit_solution(15697749564654017557)
XLA Ops:
  0.0 139.7 %shard_map.64 = bf16[1024,768]{1,0:T(8,128)(2,1)S(1)} custom-call(bf16[1024,768]{1,0:T(8,128)(2,1)} %bitcast.11, bf16[16,768]{1,0:T(8,128)(2,1)} %bitcast.12, s32[2,1024]{1,0:T(2,128)} %bitcast.13, s32[1,1024]{1,0:T(1,128)} %keep_hbm.1, bf16[768,3072]{1,0:T(8,128)(2,1)} %bitcast.9, bf16[3072,768]{1,0:T(8,128)(2,1)} %bitcast.10), custom_call_target="tpu_custom_call" | custom-call | tf_op jit(solution)/shard_map/pallas_call | solution.py:352
  139.7 1.1 copy.8

commit v6 on v5

--- a/solution.py
+++ b/solution.py
@@ -273,11 +273,15 @@
 
     first_share(0)
     local_experts(0)
-    for hosted in range(2):
+    for hosted in range(1):
         for j in far_first:
             for c in (core, 1 - core):
                 forward(hosted, j, c).start()
     first_share(1)
+    for hosted in range(1, 2):
+        for j in far_first:
+            for c in (core, 1 - core):
+                forward(hosted, j, c).start()
     second_share(0)
     remote_experts(0)
     second_share(1)

time: 141 us -> 141 us (level); the launches traced: 141 us -> 139 us
  Pallas kernels: 140 us -> 138 us
    pallas_call x1, Pallas kernels: 140 us -> 138 us  [local_layer(): pl.pallas_call(functools.partial(layer_kernel, n, groups), out_shape=pltp...]
where the time goes in v6:
time: 141 us; the launch traced here: 139 us
  Pallas kernels  138 us (98%)
    pallas_call x1, Pallas kernels, local_layer(): pl.pallas_call(functools.partial(layer_kernel, n, groups), out_shape=pltp...  138 us

profile of v6, /device:TPU:28, one launch (start us, length us, event | category | flops | bytes accessed | tf_op | source)
XLA Modules:
  0.0 139.4 jit_solution(4554314221779191451)
XLA Ops:
  0.0 138.2 %shard_map.64 = bf16[1024,768]{1,0:T(8,128)(2,1)S(1)} custom-call(bf16[1024,768]{1,0:T(8,128)(2,1)} %bitcast.11, bf16[16,768]{1,0:T(8,128)(2,1)} %bitcast.12, s32[2,1024]{1,0:T(2,128)} %bitcast.13, s32[1,1024]{1,0:T(1,128)} %keep_hbm.1, bf16[768,3072]{1,0:T(8,128)(2,1)} %bitcast.9, bf16[3072,768]{1,0:T(8,128)(2,1)} %bitcast.10), custom_call_target="tpu_custom_call" | custom-call | tf_op jit(solution)/shard_map/pallas_call | solution.py:356
  138.2 1.1 copy.8

commit v7 on v5

--- a/solution.py
+++ b/solution.py
@@ -273,11 +273,11 @@
 
     first_share(0)
     local_experts(0)
+    first_share(1)
     for hosted in range(2):
         for j in far_first:
             for c in (core, 1 - core):
                 forward(hosted, j, c).start()
-    first_share(1)
     second_share(0)
     remote_experts(0)
     second_share(1)

time: 141 us -> 142 us (level)
  no operation moved by 1% of the time
where the time goes in v7:
time: 142 us
  Pallas kernels  141 us (99%)
    pallas_call x1, Pallas kernels, local_layer(): pl.pallas_call(functools.partial(layer_kernel, n, groups), out_shape=pltp...  141 us

profile of v7, /device:TPU:28, one launch (start us, length us, event | category | flops | bytes accessed | tf_op | source)
XLA Modules:
  0.0 141.7 jit_solution(2391311626006033286)
XLA Ops:
  0.0 140.5 %shard_map.64 = bf16[1024,768]{1,0:T(8,128)(2,1)S(1)} custom-call(bf16[1024,768]{1,0:T(8,128)(2,1)} %bitcast.11, bf16[16,768]{1,0:T(8,128)(2,1)} %bitcast.12, s32[2,1024]{1,0:T(2,128)} %bitcast.13, s32[1,1024]{1,0:T(1,128)} %keep_hbm.1, bf16[768,3072]{1,0:T(8,128)(2,1)} %bitcast.9, bf16[3072,768]{1,0:T(8,128)(2,1)} %bitcast.10), custom_call_target="tpu_custom_call" | custom-call | tf_op jit(solution)/shard_map/pallas_call | solution.py:352
  140.5 1.1 copy.8
